TPU v7x, 32 devices: a whole 2x2x4 slice. The times are simulated.
32 devices in a mesh: group: 4 (over y, core), peer: 8 (over z, x).
Axes of the slice: x: 2, y: 2, z: 4, core: 2. Of those that a mesh axis runs over, the one named last changes fastest.
Arguments:
- states: float32 [41, 1048576], P(None, ('group', 'peer')), may hold values from -6 to 6
- block_part: int32 [8192], P(('group', 'peer')), may hold values from 0 to 31, as said below
- tile_perm: int32 [8192, 128], P(('group', 'peer')), may hold values from 0 to 127, each once within a row
- half_volt: float32 [40], replicated, may hold values from -4 to 4
- steepness: float32 [40], replicated, may hold values from 0.5 to 4
- gate_rate: float32 [40], replicated, may hold values from 0.1 to 1
- conductance: float32 [40], replicated, may hold values from 0.005 to 0.08
- reversal: float32 [40], replicated, may hold values from -6 to 6
Outputs:
- regrouped: float32 [41, 1048576], P(None, ('group', 'peer'))
Inputs may be any that keep to these rules, and one draw needn't show every extreme that they name: `block_part`: every partition holds exactly 256 blocks. Within each slab of 256 consecutive global blocks no partition holds more than 16 blocks; every slab has exactly 16 blocks of some partition, and every partition has exactly 16 blocks in some slab.
All inputs are finite; a program needn't handle non-finite values.
Results may differ from a plain program's by a relative error of at most 0.0001.
Values sent between devices are 32-bit elements; how exact they have to be, the bound alone decides.
A program may use at most 192 MiB of HBM per device.

v0:
```python
import jax
import jax.numpy as jnp
from jax import lax
from jax.sharding import PartitionSpec as P

time_step = 0.25


def entering(part, axis, combine, identity):
    place = lax.axis_index(axis)
    gathered = lax.all_gather(part, axis)
    state = jnp.zeros_like(part) + jnp.asarray(identity, part.dtype)

    def one(step, state):
        return combine(state, lax.dynamic_index_in_dim(gathered, step, 0, False))

    return lax.fori_loop(0, place, one, state)


def advance(state_rows, half_volt, steepness, gate_rate, conductance, reversal):
    voltage = state_rows[0:1]
    gate_vals = state_rows[1:]
    steady = jax.nn.sigmoid((voltage - half_volt[:, None]) * steepness[:, None])
    damping = jnp.exp(-gate_rate[:, None] * (1.0 + jax.nn.sigmoid(voltage)))
    gate_vals = steady + (gate_vals - steady) * damping
    current = jnp.sum(
        conductance[:, None] * gate_vals * (voltage - reversal[:, None]), axis=0, keepdims=True
    )
    voltage = voltage - time_step * current
    return jnp.concatenate([voltage, gate_vals], axis=0)


def add_counts(earlier, later):
    return earlier + later


def on_device(
    states, block_part, tile_perm, half_volt, steepness, gate_rate, conductance, reversal
):
    devices = lax.axis_size(("group", "peer"))
    local_blocks = block_part.shape[0]
    tile_width = tile_perm.shape[1]
    width = states.shape[0]
    capacity = 2 * local_blocks // devices
    partitions = jnp.arange(devices, dtype=jnp.int32)
    onehot = (block_part[:, None] == partitions[None, :]).astype(jnp.int32)
    counts = jnp.sum(onehot, axis=0, dtype=jnp.int32)
    earlier = entering(counts, ("group", "peer"), add_counts, jnp.zeros_like(counts))
    rank_in = jnp.sum(
        (jnp.cumsum(onehot, axis=0, dtype=jnp.int32) - onehot) * onehot, axis=1, dtype=jnp.int32
    )
    local_index = jnp.sum(onehot * earlier[None, :], axis=1, dtype=jnp.int32) + rank_in
    slot_index = block_part * capacity + rank_in
    requests = jnp.full((devices * capacity,), -1, jnp.int32).at[slot_index].set(local_index)
    requests = requests.reshape(devices, capacity)
    advanced = advance(states, half_volt, steepness, gate_rate, conductance, reversal)
    advanced = advanced.reshape(width, local_blocks, tile_width)
    wanted = lax.all_to_all(requests, ("group", "peer"), split_axis=0, concat_axis=0, tiled=True)
    picked = jnp.maximum(wanted, 0).reshape(-1)
    served = jnp.take(advanced, picked, axis=1)
    arrived = lax.all_to_all(
        served.reshape(width, wanted.shape[0], wanted.shape[1], tile_width),
        ("group", "peer"),
        split_axis=1,
        concat_axis=1,
        tiled=True,
    )
    flat_cols = (slot_index[:, None] * tile_width + tile_perm).reshape(-1)
    return jnp.take(arrived.reshape(width, devices * capacity * tile_width), flat_cols, axis=1)


def solution(mesh):
    return jax.shard_map(
        on_device,
        mesh=mesh,
        in_specs=(
            P(None, ("group", "peer")),
            P(("group", "peer")),
            P(("group", "peer"), None),
            P(),
            P(),
            P(),
            P(),
            P(),
        ),
        out_specs=P(None, ("group", "peer")),
        check_vma=False,
    )
```

profile of v0, /device:TPU:25, one launch (start us, length us, event | category | flops | bytes accessed | tf_op | source)
XLA Modules:
  0.0 510.8 jit_solution(10718963295124107990)
XLA Ops:
  0.0 0.8 convert_reduce_fusion
  0.8 0.2 dynamic-update-slice
  1.0 38.3 %all-reduce = s32[1024]{0:T(1024)S(1)} all-reduce(s32[1024]{0:T(1024)S(1)} %dynamic-update-slice), channel_id=2, replica_groups=mesh['group'=4,'peer'=8] {'group','peer'}, use_global_device_ids=true, to_apply=%add | all-reduce | flops 1024 | bytes 8192
  39.4 0.5 while.10
  39.9 0.7 fusion.2
  40.6 0.6 reduce-window.6
  41.2 0.2 slice_reduce_fusion
  41.4 0.8 select_reduce_fusion
  42.2 0.7 broadcast_multiply_fusion.1
  42.9 1.4 scatter_custom_fusion
  44.3 0.7 all_to_all.9
  45.0 7.2 %all-to-all-start = ((s32[32,1,16]{2,1,0:T(1,128)}), s32[32,1,16]{2,1,0:T(1,128)S(1)}, u32[]{:S(2)}, u32[]{:S(2)}) async-start(s32[32,1,16]{2,1,0:T(1,128)} %bitcast.4), calls=%async_computation | async-start | bytes 32768 | tf_op jit(solution)/shard_map/all_to_all | solution.py:58
  52.1 0.7 neg.11
  52.8 1.5 divide_add_fusion
  54.3 6.4 %multiply_reduce_fusion = (f32[32768]{0:T(1024)S(1)}, f32[40,32768]{1,0:T(8,128)S(1)}) fusion(f32[40]{0:T(128)} %param.17, f32[32768]{0:T(1024)S(1)} %bitcast.45, f32[40]{0:T(128)} %param.16, f32[32768]{0:T(1024)S(1)} %bitcast.44, f32[40]{0:T(128)S(1)} %neg.11, f32[41,32768]{1,0:T(8,128)} %param.10, f32[40]{0:T(128)} %param.14, f32[40]{0:T(128)} %param.13), kind=kLoop, calls=%fused_computation.7 | loop fusion | flops 17006592 | bytes 10879776 | tf_op jit(solution)/shard_map/reduce_sum | solution.py:26
  60.7 1.3 slice_subtract_fusion
  62.1 0.5 pad_maximum_fusion
  62.6 1.1 copy.34
  63.7 0.6 slice.21
  64.2 5.9 %copy.29 = f32[41,256,128]{2,0,1:T(8,128)} copy(f32[41,256,128]{2,1,0:T(8,128)S(1)} %slice.21) | data formatting | bytes 10747904 | tf_op jit(solution)/shard_map/reshape | solution.py:57
  70.2 0.1 copy.27
  70.4 0.1 reshape.119
  70.5 8.7 %gather_fusion = f32[512,41,128]{2,1,0:T(8,128)} fusion(f32[41,256,128]{2,0,1:T(8,128)} %copy.29, s32[1024]{0:T(1024)S(1)} %pad_clamp_fusion), kind=kCustom, calls=%fused_computation | custom fusion | bytes 21497856 | tf_op jit(solution)/shard_map/jit(_take)/gather | solution.py:60
  79.2 14.1 %copy_select_fusion = f32[41,32,16,128]{3,2,0,1:T(8,128)} fusion(f32[41,32,16,128]{3,0,2,1:T(8,128)} %bitcast.41, pred[32,16]{1,0:T(8,128)(4,1)S(1)} %copy.27), kind=kLoop, calls=%fused_computation.5 | loop fusion | flops 2686976 | bytes 21496320 | tf_op jit(solution)/shard_map/jit(_take)/select_n | solution.py:60
  93.3 5.9 %all-to-all-start.1 = ((f32[41,32,16,128]{3,2,0,1:T(8,128)}), f32[41,32,16,128]{3,2,0,1:T(8,128)}, u32[]{:S(2)}, u32[]{:S(2)}) async-start(f32[41,32,16,128]{3,2,0,1:T(8,128)} %copy_select_fusion), calls=%async_computation.1 | async-start | bytes 21495808 | tf_op jit(solution)/shard_map/all_to_all | solution.py:61
  99.2 0.1 compare_and_fusion
  99.3 0.1 compare_select_fusion
  99.5 240.6 %all-to-all-done.1 = f32[41,32,16,128]{3,2,0,1:T(8,128)} async-done(((f32[41,32,16,128]{3,2,0,1:T(8,128)}), f32[41,32,16,128]{3,2,0,1:T(8,128)}, u32[]{:S(2)}, u32[]{:S(2)}) %all-to-all-start.1) | async-done | bytes 10747936 | tf_op jit(solution)/shard_map/all_to_all | solution.py:61
  340.0 20.7 %copy.31 = f32[41,32,16,128]{0,3,2,1:T(8,128)} copy(f32[41,32,16,128]{3,2,0,1:T(8,128)} %all-to-all-done.1) | data formatting | bytes 21495808 | tf_op jit(solution)/shard_map/all_to_all | solution.py:61
  360.8 118.8 %gather_fusion.1 = f32[32768,41]{1,0:T(8,128)} fusion(f32[41,65536]{0,1:T(8,128)} %bitcast.40, s32[32768]{0:T(1024)S(1)} %broadcast_clamp_fusion), kind=kCustom, calls=%fused_computation.1 | custom fusion | bytes 10878976 | tf_op jit(solution)/shard_map/jit(_take)/gather | solution.py:69
  479.6 19.1 %select_bitcast_fusion = f32[41,32768]{0,1:T(8,128)} fusion(f32[32768,41]{1,0:T(8,128)} %gather_fusion.1, pred[32768]{0:T(1024)(128)(4,1)S(1)} %get-tuple-element.39), kind=kLoop, calls=%fused_computation.4 | loop fusion | flops 1343488 | bytes 10780672 | tf_op jit(solution)/shard_map/jit(_take)/select_n | solution.py:69
  498.7 12.1 %copy.32 = f32[41,32768]{1,0:T(8,128)} copy(f32[41,32768]{0,1:T(8,128)} %select_bitcast_fusion) | data formatting | bytes 10747904 | tf_op jit(solution)/shard_map/jit(_take)/select_n | solution.py:69
  (29 shorter events, 0.5 us)
Async XLA Ops:
  45.0 25.2 %all-to-all-start = ((s32[32,1,16]{2,1,0:T(1,128)}), s32[32,1,16]{2,1,0:T(1,128)S(1)}, u32[]{:S(2)}, u32[]{:S(2)}) async-start(s32[32,1,16]{2,1,0:T(1,128)} %bitcast.4), calls=%async_computation | async-start | bytes 32768 | tf_op jit(solution)/shard_map/all_to_all | solution.py:58
  93.3 5.9 %copy-start = (s32[256,128]{1,0:T(8,128)S(1)}, s32[256,128]{1,0:T(8,128)}, u32[]{:S(2)}) copy-start(s32[256,128]{1,0:T(8,128)} %param.12) | copy-start | bytes 393220
  93.3 246.8 %all-to-all-start.1 = ((f32[41,32,16,128]{3,2,0,1:T(8,128)}), f32[41,32,16,128]{3,2,0,1:T(8,128)}, u32[]{:S(2)}, u32[]{:S(2)}) async-start(f32[41,32,16,128]{3,2,0,1:T(8,128)} %copy_select_fusion), calls=%async_computation.1 | async-start | bytes 21495808 | tf_op jit(solution)/shard_map/all_to_all | solution.py:61
where the time goes:
time: 512 us; the launch traced here: 511 us
  waiting for transfers between devices  241 us (47%)
  local copies, waits for them, and re-layouts  171 us (33%)
  other arithmetic  47.6 us (9%)
  blocking collectives  38.3 us (7%)
  starting transfers between devices  13 us (3%)
    all_to_all x1, waiting for transfers between devices, on_device(): lax.all_to_all(served.reshape(width, wanted.shape[0], wanted.shape[1], ti...  241 us
    gather x1, local copies, waits for them, and re-layouts, on_device(): jnp.take(arrived.reshape(width, devices * capacity * tile_width), flat_co...  119 us
    unnamed x1, blocking collectives  38.3 us
    all_to_all x1, local copies, waits for them, and re-layouts, on_device(): lax.all_to_all(served.reshape(width, wanted.shape[0], wanted.shape[1], ti...  20.7 us
    select_n x2, other arithmetic, on_device(): jnp.take(arrived.reshape(width, devices * capacity * tile_width), flat_co...  19.2 us
    select_n x1, other arithmetic, on_device(): served = jnp.take(advanced, picked, axis=1)  14.1 us
    select_n x1, local copies, waits for them, and re-layouts, on_device(): jnp.take(arrived.reshape(width, devices * capacity * tile_width), flat_co...  12.1 us
  transfers between devices with their start and end apart: 2, of which 1 were waited for; matrix products, arithmetic and copies ran while one was open for 4% of the time, Pallas kernels for 0%

commit v1 on v0

v1 whole, which is shorter than its diff:
```python
import functools
import jax
import jax.numpy as jnp
import numpy as np
from jax import lax
from jax.experimental import pallas as pl
from jax.experimental.pallas import tpu as pltpu
from jax.sharding import PartitionSpec as P

time_step = 0.25
LANES = 128
ROWS = 8
MESH_ID = pl.DeviceIdType.MESH
VMEM_LIMIT = 67043328
SLOTS = 192
ORDERS = ((2, 1, 4, 0, 3), (0, 4, 3, 2, 1))


def submasks(bits):
    masks = [0]
    for bit in bits:
        masks = masks + [m | (1 << bit) for m in masks]
    return sorted(masks)


def stage_pairs(order, j):
    before, after = order[:j], order[j + 1 :]
    here = 1 << order[j]
    return [(a, b | here) for a in submasks(before) for b in submasks(after)]


def flip(d, mask):
    out = d
    bit = 0
    while (1 << bit) <= mask:
        if mask & (1 << bit):
            out = out + (1 - 2 * ((d // (1 << bit)) % 2)) * (1 << bit)
        bit += 1
    return out


def my_index(peers):
    return lax.axis_index("group") * peers + lax.axis_index("peer")


def counts_kernel(devices, peers, x_ref, out_ref, send_sem, recv_sem, local_sem):
    d = my_index(peers)
    barrier = pltpu.get_barrier_semaphore()
    for k in range(1, devices):
        to = (d + k) % devices
        pl.semaphore_signal(
            barrier, inc=1, device_id=(to // peers, to % peers), device_id_type=MESH_ID
        )
    pl.semaphore_wait(barrier, devices - 1)
    own = pltpu.make_async_copy(x_ref.at[0], out_ref.at[d], local_sem)
    own.start()
    for k in range(1, devices):
        to = (d + k) % devices
        pltpu.make_async_remote_copy(
            src_ref=x_ref.at[0], dst_ref=out_ref.at[d],
            send_sem=send_sem.at[k], recv_sem=recv_sem.at[k],
            device_id=(to // peers, to % peers), device_id_type=MESH_ID,
        ).start()
    own.wait()
    for k in range(1, devices):
        src = (d + devices - k) % devices
        pltpu.make_async_remote_copy(
            src_ref=x_ref.at[0], dst_ref=out_ref.at[src],
            send_sem=send_sem.at[k], recv_sem=recv_sem.at[k],
            device_id=(src // peers, src % peers), device_id_type=MESH_ID,
        ).wait()


def gather_counts(row, devices, peers):
    return pl.pallas_call(
        functools.partial(counts_kernel, devices, peers),
        out_shape=jax.ShapeDtypeStruct((devices, 1, LANES), jnp.int32),
        in_specs=[pl.BlockSpec(memory_space=pltpu.VMEM)],
        out_specs=pl.BlockSpec(memory_space=pltpu.VMEM),
        scratch_shapes=[
            pltpu.SemaphoreType.DMA((devices,)),
            pltpu.SemaphoreType.DMA((devices,)),
            pltpu.SemaphoreType.DMA,
        ],
        compiler_params=pltpu.CompilerParams(collective_id=0, has_side_effects=True),
    )(row)


def table_kernel(
    devices, peers, own_blocks, slots, c_ref, part_ref, tables_ref, final_ref, earlier
):
    d = my_index(peers)
    pool_size = own_blocks + len(ORDERS[0]) * slots
    run = jnp.int32(0)
    for s in range(devices):
        earlier[s] = run
        run = run + c_ref[s, 0, d]
    shape = (ROWS, LANES)
    flat = lax.broadcasted_iota(jnp.int32, shape, 0) * LANES + lax.broadcasted_iota(
        jnp.int32, shape, 1
    )
    tables_ref[...] = jnp.zeros_like(tables_ref)
    part = part_ref[...]
    sources = lax.broadcasted_iota(jnp.int32, (devices, own_blocks), 0)
    onehot = part == sources
    onehot_f = onehot.astype(jnp.float32)
    upper = (
        lax.broadcasted_iota(jnp.int32, (own_blocks, own_blocks), 0)
        < lax.broadcasted_iota(jnp.int32, (own_blocks, own_blocks), 1)
    ).astype(jnp.float32)
    rank = jnp.dot(onehot_f, upper, preferred_element_type=jnp.float32).astype(jnp.int32)
    near = lax.broadcasted_iota(jnp.int32, (devices, LANES), 0)
    final_ref[...] = jnp.zeros_like(final_ref)
    for o, order in enumerate(ORDERS):
        pos = {(0, m): earlier[flip(d, m)] for m in range(devices)}
        for j, bit in enumerate(order):
            pairs = stage_pairs(order, j)
            table = flat
            start = jnp.int32(0)
            shift = jnp.int32(0)
            for a, b in pairs:
                now = pos[(a, b)] - start
                table = table + jnp.where(flat >= start, now - shift, 0)
                shift = now
                start = start + c_ref[flip(d, b), 0, flip(d, a)]
            table = jnp.where(flat < start, table, 0)
            row = (o * len(order) + j) * 2
            tables_ref[row : row + 2, :] = table[0:2]
            fresh = {
                k: v for k, v in pos.items() if not (k[1] >> bit) & 1
            }
            partner = flip(d, 1 << bit)
            start = jnp.int32(own_blocks + j * slots)
            for a, b in pairs:
                fresh[(a | (1 << bit), b ^ (1 << bit))] = start
                start = start + c_ref[flip(partner, b), 0, flip(partner, a)]
            pos = fresh
        base = jnp.zeros((devices, LANES), jnp.int32)
        for a in range(devices):
            base = jnp.where(near == flip(d, a), pos[(a, 0)], base)
        whole = jnp.sum(jnp.where(onehot, base[:, 0:1] + rank, 0), axis=0, keepdims=True)
        whole = jnp.clip(whole, 0, pool_size - 1)
        final_ref[o : o + 1, :] = whole


def make_tables(counts, part, devices, peers, own_blocks, slots):
    return pl.pallas_call(
        functools.partial(table_kernel, devices, peers, own_blocks, slots),
        out_shape=(
            jax.ShapeDtypeStruct((24, LANES), jnp.int32),
            jax.ShapeDtypeStruct((8, own_blocks), jnp.int32),
        ),
        in_specs=[
            pl.BlockSpec(memory_space=pltpu.SMEM),
            pl.BlockSpec(memory_space=pltpu.VMEM),
        ],
        out_specs=(
            pl.BlockSpec(memory_space=pltpu.VMEM),
            pl.BlockSpec(memory_space=pltpu.VMEM),
        ),
        scratch_shapes=[pltpu.SMEM((devices,), jnp.int32)],
    )(counts, part)


def largest_load(counts, devices):
    ids = np.arange(devices)
    apart = ids[:, None] ^ ids[None, :]
    to_rows, from_rows = [], []
    for order in ORDERS:
        for j, bit in enumerate(order):
            before = sum(1 << b for b in order[:j])
            after = sum(1 << b for b in order[j + 1 :])
            here = 1 << bit
            to_rows.append(((apart & before) == 0) & ((apart & here) != 0))
            from_rows.append((apart & (here | after)) == 0)
    to_rows = jnp.asarray(np.concatenate(to_rows), jnp.bfloat16)
    from_rows = jnp.asarray(np.concatenate(from_rows), jnp.float32)
    part = jnp.dot(
        to_rows, counts.astype(jnp.bfloat16), preferred_element_type=jnp.float32
    )
    return jnp.max(jnp.sum(part * from_rows, axis=1)).astype(jnp.int32)


EVENTS = (
    (0, 0), (3, 0), (1, 0), (4, 0), (5, 0), (3, 1), (5, 1), (0, 1), (2, 0), (4, 1),
    (3, 2), (5, 2), (1, 1), (3, 3), (0, 2), (4, 2), (0, 3), (2, 1), (4, 3), (1, 2),
    (0, 4), (5, 3), (1, 3), (0, 5), (3, 4), (2, 2), (1, 4), (2, 3), (1, 5), (2, 4),
    (2, 5), (5, 4), (4, 4), (3, 5), (5, 5), (4, 5),
)
CHUNK_ORDER = (0, 0, 0, 1, 1, 1)
BUFFERS = {2: (0, 1), 1: (2, 3), 0: (4, 5), 4: (6,), 3: (7,)}


def exchange_kernel(
    peers, own_blocks, slots, unroll,
    tables, finals, params, states, out, out_row,
    pool, pool_row, landed, landed_row, packed, packed_row, ready, ready_row,
    send_sem, recv_sem, out_sem,
):
    d = my_index(peers)
    barrier = pltpu.get_barrier_semaphore()
    bits = sorted(ORDERS[0])
    for bit in bits:
        to = flip(d, 1 << bit)
        pl.semaphore_signal(
            barrier, inc=1, device_id=(to // peers, to % peers), device_id_type=MESH_ID
        )

    tiles = pool.shape[0]

    def advance_block(b):
        cols = pl.ds(pl.multiple_of(b * LANES, LANES), LANES)
        top = states[0:ROWS, cols]
        voltage = top[0:1, :]
        spread = jnp.broadcast_to(voltage, (ROWS, LANES))
        slow = -(1.0 + jax.nn.sigmoid(spread))

        def gates(vals, base, count):
            half, steep, rate, cond, rev = (
                params[k, base : base + count, :] for k in range(5)
            )
            v = spread[0:count]
            steady = jax.nn.sigmoid((v - half) * steep)
            damping = jnp.exp(rate * slow[0:count])
            new = steady + (vals - steady) * damping
            return new, cond * new * (v - rev)

        total = jnp.zeros((ROWS, LANES), jnp.float32)
        for t in range(1, tiles):
            new, term = gates(states[t * ROWS : (t + 1) * ROWS, cols], t * ROWS, ROWS)
            pool[t, b] = new
            total = total + term
        last = tiles * ROWS
        new_row, term_row = gates(states[last : last + 1, cols], last, 1)
        pool_row[pl.ds(b, 1), :] = new_row
        new, term = gates(top, 0, ROWS)
        total = total + term
        current = jnp.sum(total, axis=0, keepdims=True) + term_row
        moved = voltage - time_step * current
        first = lax.broadcasted_iota(jnp.int32, (ROWS, LANES), 0) == 0
        pool[0, b] = jnp.where(first, jnp.broadcast_to(moved, (ROWS, LANES)), new)

    def advance_loop(i, _):
        for u in range(4):
            advance_block(i * 4 + u)
        return 0

    lax.fori_loop(0, own_blocks // 4, advance_loop, 0)
    pl.semaphore_wait(barrier, len(bits))

    stages = len(bits)
    used = {}
    copies = {}
    outs = []
    turn = {bit: 0 for bit in bits}

    def arrive(c, j):
        copies[(c, j)].wait_recv()
        base = own_blocks + j * slots

        def move(i, _):
            for u in range(unroll):
                k = i * unroll + u
                if c < tiles:
                    pool[c, base + k] = landed[c, j, k]
            return 0

        if c < tiles:
            lax.fori_loop(0, slots // unroll, move, 0)
        else:
            pool_row[base : base + slots, :] = landed_row[j]

    for c, j in EVENTS:
        order = ORDERS[CHUNK_ORDER[c]]
        if j > 0:
            arrive(c, j - 1)
        if j < stages:
            bit = order[j]
            if c < tiles:
                names = BUFFERS[bit]
                buf = names[turn[bit] % len(names)]
                turn[bit] += 1
                if buf in used:
                    copies[used[buf]].wait_send()
                used[buf] = (c, j)
            row = (CHUNK_ORDER[c] * stages + j) * 2 * LANES

            def pack(i, _):
                for u in range(unroll):
                    k = i * unroll + u
                    at = tables[row + k]
                    if c < tiles:
                        packed[buf, k] = pool[c, at]
                    else:
                        packed_row[j, pl.ds(k, 1), :] = pool_row[pl.ds(at, 1), :]
                return 0

            lax.fori_loop(0, slots // unroll, pack, 0)
            to = flip(d, 1 << bit)
            copy = pltpu.make_async_remote_copy(
                src_ref=packed.at[buf] if c < tiles else packed_row.at[j],
                dst_ref=landed.at[c, j] if c < tiles else landed_row.at[j],
                send_sem=send_sem.at[c, j],
                recv_sem=recv_sem.at[c, j],
                device_id=(to // peers, to % peers),
                device_id_type=MESH_ID,
            )
            copy.start()
            copies[(c, j)] = copy
        else:
            if c < tiles and outs:
                outs.pop().wait()
            first = CHUNK_ORDER[c] * own_blocks

            def pick(i, _):
                for u in range(unroll):
                    k = i * unroll + u
                    at = finals[first + k]
                    if c < tiles:
                        ready[k] = pool[c, at]
                    else:
                        ready_row[pl.ds(k, 1), :] = pool_row[pl.ds(at, 1), :]
                return 0

            lax.fori_loop(0, own_blocks // unroll, pick, 0)
            if c < tiles:
                copy = pltpu.make_async_copy(ready, out.at[c], out_sem.at[0])
                copy.start()
                outs.append(copy)
            else:
                row_copy = pltpu.make_async_copy(ready_row, out_row, out_sem.at[1])
                row_copy.start()
    row_copy.wait()
    for copy in outs:
        copy.wait()
    last_use = set(used.values()) | {(tiles, j) for j in range(stages)}
    for key in sorted(last_use):
        copies[key].wait_send()


def exchange(tables, finals, params, states, peers, own_blocks, slots):
    tiles = states.shape[0] // ROWS
    stages = len(ORDERS[0])
    size = own_blocks + stages * slots
    f32 = jnp.float32
    return pl.pallas_call(
        functools.partial(exchange_kernel, peers, own_blocks, slots, 8),
        out_shape=(
            jax.ShapeDtypeStruct((tiles, own_blocks, ROWS, LANES), f32),
            jax.ShapeDtypeStruct((own_blocks, LANES), f32),
        ),
        in_specs=[
            pl.BlockSpec(memory_space=pltpu.SMEM),
            pl.BlockSpec(memory_space=pltpu.SMEM),
            pl.BlockSpec(memory_space=pltpu.VMEM),
            pl.BlockSpec(memory_space=pltpu.VMEM),
        ],
        out_specs=(
            pl.BlockSpec(memory_space=pl.ANY),
            pl.BlockSpec(memory_space=pl.ANY),
        ),
        scratch_shapes=[
            pltpu.VMEM((tiles, size, ROWS, LANES), f32),
            pltpu.VMEM((size, LANES), f32),
            pltpu.VMEM((tiles, stages, slots, ROWS, LANES), f32),
            pltpu.VMEM((stages, slots, LANES), f32),
            pltpu.VMEM((8, slots, ROWS, LANES), f32),
            pltpu.VMEM((stages, slots, LANES), f32),
            pltpu.VMEM((own_blocks, ROWS, LANES), f32),
            pltpu.VMEM((own_blocks, LANES), f32),
            pltpu.SemaphoreType.DMA((tiles + 1, stages)),
            pltpu.SemaphoreType.DMA((tiles + 1, stages)),
            pltpu.SemaphoreType.DMA((2,)),
        ],
        compiler_params=pltpu.CompilerParams(
            collective_id=1, has_side_effects=True, vmem_limit_bytes=VMEM_LIMIT
        ),
    )(tables, finals, params, states)


def place_kernel(tiles, blocks, got, got_row, perm, out):
    for group in range(blocks // ROWS):
        rows = slice(group * ROWS, (group + 1) * ROWS)
        turned = jnp.take_along_axis(
            got_row[rows, :], perm[rows, :], axis=1, mode="promise_in_bounds"
        )
        for u in range(ROWS):
            b = group * ROWS + u
            cols = slice(b * LANES, (b + 1) * LANES)
            where = jnp.broadcast_to(perm[b : b + 1, :], (ROWS, LANES))
            for t in range(tiles):
                out[t * ROWS : (t + 1) * ROWS, cols] = jnp.take_along_axis(
                    got[t, b], where, axis=1, mode="promise_in_bounds"
                )
            out[tiles * ROWS : tiles * ROWS + 1, cols] = turned[u : u + 1, :]


def place(got, got_row, perm, width, own_blocks):
    tiles = got.shape[0]
    step = 32
    return pl.pallas_call(
        functools.partial(place_kernel, tiles, step),
        grid=(own_blocks // step,),
        out_shape=jax.ShapeDtypeStruct((width, own_blocks * LANES), jnp.float32),
        in_specs=[
            pl.BlockSpec((tiles, step, ROWS, LANES), lambda i: (0, i, 0, 0)),
            pl.BlockSpec((step, LANES), lambda i: (i, 0)),
            pl.BlockSpec((step, LANES), lambda i: (i, 0)),
        ],
        out_specs=pl.BlockSpec((width, step * LANES), lambda i: (0, i)),
    )(got, got_row, perm)


def advance(state_rows, half_volt, steepness, gate_rate, conductance, reversal):
    voltage = state_rows[0:1]
    gate_vals = state_rows[1:]
    steady = jax.nn.sigmoid((voltage - half_volt[:, None]) * steepness[:, None])
    damping = jnp.exp(-gate_rate[:, None] * (1.0 + jax.nn.sigmoid(voltage)))
    gate_vals = steady + (gate_vals - steady) * damping
    current = jnp.sum(
        conductance[:, None] * gate_vals * (voltage - reversal[:, None]), axis=0, keepdims=True
    )
    voltage = voltage - time_step * current
    return jnp.concatenate([voltage, gate_vals], axis=0)


def general(counts_all, devices, states, block_part, tile_perm, *gate_params):
    d = lax.axis_index(("group", "peer"))
    local_blocks = block_part.shape[0]
    tile_width = tile_perm.shape[1]
    width = states.shape[0]
    capacity = 2 * local_blocks // devices
    partitions = jnp.arange(devices, dtype=jnp.int32)
    onehot = (block_part[:, None] == partitions[None, :]).astype(jnp.int32)
    before = (partitions < d).astype(jnp.int32)
    earlier = jnp.sum(counts_all * before[:, None], axis=0, dtype=jnp.int32)
    rank_in = jnp.sum(
        (jnp.cumsum(onehot, axis=0, dtype=jnp.int32) - onehot) * onehot, axis=1, dtype=jnp.int32
    )
    local_index = jnp.sum(onehot * earlier[None, :], axis=1, dtype=jnp.int32) + rank_in
    slot_index = block_part * capacity + rank_in
    requests = jnp.full((devices * capacity,), -1, jnp.int32).at[slot_index].set(local_index)
    requests = requests.reshape(devices, capacity)
    advanced = advance(states, *gate_params)
    advanced = advanced.reshape(width, local_blocks, tile_width)
    wanted = lax.all_to_all(requests, ("group", "peer"), split_axis=0, concat_axis=0, tiled=True)
    picked = jnp.maximum(wanted, 0).reshape(-1)
    served = jnp.take(advanced, picked, axis=1)
    arrived = lax.all_to_all(
        served.reshape(width, wanted.shape[0], wanted.shape[1], tile_width),
        ("group", "peer"), split_axis=1, concat_axis=1, tiled=True,
    )
    flat_cols = (slot_index[:, None] * tile_width + tile_perm).reshape(-1)
    return jnp.take(arrived.reshape(width, devices * capacity * tile_width), flat_cols, axis=1)


def on_device(devices, peers, states, block_part, tile_perm, *gate_params):
    own_blocks = block_part.shape[0]
    width = states.shape[0]
    partitions = jnp.arange(LANES, dtype=jnp.int32)
    counts = jnp.sum(
        (block_part[:, None] == partitions[None, :]).astype(jnp.int32), axis=0, dtype=jnp.int32
    )
    if devices != 1 << len(ORDERS[0]) or width % ROWS != 1:
        gathered = lax.all_gather(counts[:devices], ("group", "peer"))
        return general(gathered, devices, states, block_part, tile_perm, *gate_params)
    gathered = gather_counts(counts.reshape(1, 1, LANES), devices, peers)
    matrix = gathered[:, 0, :devices]
    fits = largest_load(matrix, devices) <= SLOTS
    tables, finals = make_tables(
        gathered, block_part.reshape(1, own_blocks), devices, peers, own_blocks, SLOTS
    )
    table_list = tables.reshape(-1)
    final_list = finals[0:2].reshape(-1)
    padded = jnp.stack([jnp.pad(p, (1, 0)) for p in gate_params])
    params = jnp.broadcast_to(padded[:, :, None], padded.shape + (LANES,))

    def fast():
        got, got_row = exchange(
            table_list, final_list, params, states, peers, own_blocks, SLOTS
        )
        return place(got, got_row, tile_perm, width, own_blocks)

    def slow():
        return general(matrix, devices, states, block_part, tile_perm, *gate_params)

    return lax.cond(fits, fast, slow)


def solution(mesh):
    both = P(("group", "peer"))
    return jax.shard_map(
        functools.partial(on_device, mesh.devices.size, mesh.shape["peer"]),
        mesh=mesh,
        in_specs=(P(None, ("group", "peer")), both, P(("group", "peer"), None)) + (P(),) * 5,
        out_specs=P(None, ("group", "peer")),
        check_vma=False,
    )
```

time: 512 us -> 257 us (0.50)
  Pallas kernels: 0 us -> 245 us
  waiting for transfers between devices: 241 us -> 0 us
  local copies, waits for them, and re-layouts: 171 us -> 3.58 us
  other arithmetic: 47.6 us -> 1.91 us
  blocking collectives: 38.3 us -> 0 us
  starting transfers between devices: 13 us -> 0 us
    pallas_call x0 -> x4, Pallas kernels: none -> 245 us  [the longest x1 225 us: exchange(): pl.pallas_call(functools.partial(exchange_kernel, peers, own_blocks, slot...]
    all_to_all x2 -> x0, waiting for transfers between devices: 241 us -> none  [the longest x1 241 us: on_device(): lax.all_to_all(served.reshape(width, wanted.shape[0], wanted.shape[1], ti...]
    gather x2 -> x0, local copies, waits for them, and re-layouts: 128 us -> none  [the longest x1 119 us: on_device(): jnp.take(arrived.reshape(width, devices * capacity * tile_width), flat_co...]
    unnamed x1 -> x0, blocking collectives: 38.3 us -> none
    select_n x3 -> x0, other arithmetic: 33.3 us -> none  [the longest x2 19.2 us: on_device(): jnp.take(arrived.reshape(width, devices * capacity * tile_width), flat_co...]
    all_to_all x3 -> x0, local copies, waits for them, and re-layouts: 21.5 us -> none  [the longest x1 20.7 us: on_device(): lax.all_to_all(served.reshape(width, wanted.shape[0], wanted.shape[1], ti...]
    all_to_all x2 -> x0, starting transfers between devices: 13 us -> none  [the longest x1 7.17 us: on_device(): lax.all_to_all(requests, ('group', 'peer'), split_axis=0, concat_axis=0,...]
    select_n x1 -> x0, local copies, waits for them, and re-layouts: 12.1 us -> none  [on_device(): jnp.take(arrived.reshape(width, devices * capacity * tile_width), flat_co...]
  transfers between devices with their start and end apart: 2 -> 0, of which waited for: 1 -> 0; matrix products, arithmetic and copies ran while one was open for 4% -> 0% of each run, Pallas kernels for 0% -> 0%
where the time goes in v1:
time: 257 us; the launch traced here: 252 us
  Pallas kernels  245 us (95%)
  local copies, waits for them, and re-layouts  3.58 us (1%)
    pallas_call x1, Pallas kernels, exchange(): pl.pallas_call(functools.partial(exchange_kernel, peers, own_blocks, slot...  225 us
    pallas_call x1, Pallas kernels, gather_counts(): pl.pallas_call(functools.partial(counts_kernel, devices, peers), out_shap...  8.77 us
    pallas_call x1, Pallas kernels, place(): pl.pallas_call(functools.partial(place_kernel, tiles, step), grid=(own_bl...  8.35 us

profile of v1, /device:TPU:25, one launch (start us, length us, event | category | flops | bytes accessed | tf_op | source)
XLA Modules:
  0.0 251.8 jit_solution(3149327216767565507)
XLA Ops:
  0.0 0.7 pad_bitcast_fusion.4
  0.7 1.3 convert_reduce_fusion
  2.0 0.7 pad_bitcast_fusion.2
  2.8 0.7 pad_bitcast_fusion
  3.6 8.8 %shard_map.102.c_ref = s32[32,1,128]{2,1,0:T(1,128)S(1)} custom-call(s32[1,1,128]{2,1,0:T(1,128)} %bitcast.77), custom_call_target="tpu_custom_call" | custom-call | tf_op jit(solution)/shard_map/pallas_call | solution.py:75
  12.3 1.1 fusion.6
  13.4 0.6 reduce_max.9
  14.7 2.3 shard_map.103
  17.0 234.8 %conditional.1 = (f32[41,32768]{1,0:T(8,128)}) conditional(s32[]{:T(128)} %convert_element_type.35, (s32[256]{0:T(256)}, s32[256,128]{1,0:T(8,128)}, s32[32,32]{1,0:T(8,128)S(1)}, f32[41,32768]{1,0:T(8,128)}, f32[40]{0:T(128)}, /*index=5*/f32[40]{0:T(128)}, f32[40]{0:T(128)}, f32[40]{0:T(128)}, f32[40]{0:T(128)}) %tuple.33, (s32[24,128]{1,0:T(8,128)}, ...), branch_computations={%region_3.11_spmd, %region_11.12_spmd} | conditional | flops 24065960 | bytes 187456160 | solution.py:487
  17.0 0.6 copy.54
  17.6 0.7 broadcast_in_dim.18.params
  18.4 225.1 %branch_1_fun.2 = (f32[5,256,8,128]{3,2,1,0:T(8,128)}, f32[256,128]{1,0:T(8,128)}) custom-call(s32[3072]{0:T(1024)} %bitcast.14.tables, s32[512]{0:T(512)} %bitcast.76, f32[5,41,128]{2,1,0:T(8,128)} %broadcast_in_dim.18.params, f32[41,32768]{1,0:T(8,128)} %get-tuple-element.52.states), custom_call_target="tpu_custom_call" | custom-call | tf_op jit(solution)/shard_map/cond/branch_1_fun/pallas_call | solution.py:346
  243.5 8.4 %branch_1_fun.3 = f32[41,32768]{1,0:T(8,128)} custom-call(f32[5,256,8,128]{3,2,1,0:T(8,128)} %get-tuple-element.53.got, f32[256,128]{1,0:T(8,128)} %get-tuple-element.54.got_row, s32[256,128]{1,0:T(8,128)} %get-tuple-element.55.perm), custom_call_target="tpu_custom_call" | custom-call | tf_op jit(solution)/shard_map/cond/branch_1_fun/pallas_call | solution.py:401
  (2 shorter events, 0.0 us)

commit v2 on v1

--- a/solution.py
+++ b/solution.py
@@ -12,8 +12,8 @@
 ROWS = 8
 MESH_ID = pl.DeviceIdType.MESH
 VMEM_LIMIT = 67043328
-SLOTS = 192
-ORDERS = ((2, 1, 4, 0, 3), (0, 4, 3, 2, 1))
+SLOTS = (184, 208, 216, 200, 184)
+ORDERS = ((2, 1, 4, 0, 3), (1, 2, 4, 0, 3), (0, 4, 3, 2, 1), (0, 4, 3, 1, 2))
 
 
 def submasks(bits):
@@ -90,7 +90,7 @@
     devices, peers, own_blocks, slots, c_ref, part_ref, tables_ref, final_ref, earlier
 ):
     d = my_index(peers)
-    pool_size = own_blocks + len(ORDERS[0]) * slots
+    pool_size = own_blocks + sum(slots)
     run = jnp.int32(0)
     for s in range(devices):
         earlier[s] = run
@@ -99,7 +99,6 @@
     flat = lax.broadcasted_iota(jnp.int32, shape, 0) * LANES + lax.broadcasted_iota(
         jnp.int32, shape, 1
     )
-    tables_ref[...] = jnp.zeros_like(tables_ref)
     part = part_ref[...]
     sources = lax.broadcasted_iota(jnp.int32, (devices, own_blocks), 0)
     onehot = part == sources
@@ -130,7 +129,7 @@
                 k: v for k, v in pos.items() if not (k[1] >> bit) & 1
             }
             partner = flip(d, 1 << bit)
-            start = jnp.int32(own_blocks + j * slots)
+            start = jnp.int32(own_blocks + sum(slots[:j]))
             for a, b in pairs:
                 fresh[(a | (1 << bit), b ^ (1 << bit))] = start
                 start = start + c_ref[flip(partner, b), 0, flip(partner, a)]
@@ -147,7 +146,7 @@
     return pl.pallas_call(
         functools.partial(table_kernel, devices, peers, own_blocks, slots),
         out_shape=(
-            jax.ShapeDtypeStruct((24, LANES), jnp.int32),
+            jax.ShapeDtypeStruct((2 * len(ORDERS) * len(slots), LANES), jnp.int32),
             jax.ShapeDtypeStruct((8, own_blocks), jnp.int32),
         ),
         in_specs=[
@@ -162,10 +161,10 @@
     )(counts, part)
 
 
-def largest_load(counts, devices):
+def messages_fit(counts, devices):
     ids = np.arange(devices)
     apart = ids[:, None] ^ ids[None, :]
-    to_rows, from_rows = [], []
+    to_rows, from_rows, room = [], [], []
     for order in ORDERS:
         for j, bit in enumerate(order):
             before = sum(1 << b for b in order[:j])
@@ -173,21 +172,23 @@
             here = 1 << bit
             to_rows.append(((apart & before) == 0) & ((apart & here) != 0))
             from_rows.append((apart & (here | after)) == 0)
+            room.append(np.full((devices,), SLOTS[j]))
     to_rows = jnp.asarray(np.concatenate(to_rows), jnp.bfloat16)
     from_rows = jnp.asarray(np.concatenate(from_rows), jnp.float32)
     part = jnp.dot(
         to_rows, counts.astype(jnp.bfloat16), preferred_element_type=jnp.float32
     )
-    return jnp.max(jnp.sum(part * from_rows, axis=1)).astype(jnp.int32)
+    room = jnp.asarray(np.concatenate(room), jnp.float32)
+    return jnp.max(jnp.sum(part * from_rows, axis=1) - room) <= 0.0
 
 
 EVENTS = (
-    (0, 0), (3, 0), (1, 0), (4, 0), (5, 0), (3, 1), (5, 1), (0, 1), (2, 0), (4, 1),
-    (3, 2), (5, 2), (1, 1), (3, 3), (0, 2), (4, 2), (0, 3), (2, 1), (4, 3), (1, 2),
-    (0, 4), (5, 3), (1, 3), (0, 5), (3, 4), (2, 2), (1, 4), (2, 3), (1, 5), (2, 4),
-    (2, 5), (5, 4), (4, 4), (3, 5), (5, 5), (4, 5),
+    (1, 0), (0, 0), (3, 0), (4, 0), (5, 0), (3, 1), (5, 1), (0, 1), (1, 1), (4, 1),
+    (3, 2), (5, 2), (4, 2), (2, 0), (3, 3), (0, 2), (1, 2), (4, 3), (0, 3), (1, 3),
+    (0, 4), (1, 4), (2, 1), (3, 4), (5, 3), (0, 5), (1, 5), (4, 4), (2, 2), (5, 4),
+    (2, 3), (2, 4), (2, 5), (3, 5), (5, 5), (4, 5),
 )
-CHUNK_ORDER = (0, 0, 0, 1, 1, 1)
+CHUNK_ORDER = (0, 1, 1, 2, 3, 2)
 BUFFERS = {2: (0, 1), 1: (2, 3), 0: (4, 5), 4: (6,), 3: (7,)}
 
 
@@ -256,19 +257,20 @@
 
     def arrive(c, j):
         copies[(c, j)].wait_recv()
-        base = own_blocks + j * slots
+        begin = sum(slots[:j])
+        base = own_blocks + begin
 
         def move(i, _):
             for u in range(unroll):
                 k = i * unroll + u
                 if c < tiles:
-                    pool[c, base + k] = landed[c, j, k]
+                    pool[c, base + k] = landed[c, begin + k]
             return 0
 
         if c < tiles:
-            lax.fori_loop(0, slots // unroll, move, 0)
+            lax.fori_loop(0, slots[j] // unroll, move, 0)
         else:
-            pool_row[base : base + slots, :] = landed_row[j]
+            pool_row[base : base + slots[j], :] = landed_row[begin : begin + slots[j], :]
 
     for c, j in EVENTS:
         order = ORDERS[CHUNK_ORDER[c]]
@@ -283,6 +285,7 @@
                 if buf in used:
                     copies[used[buf]].wait_send()
                 used[buf] = (c, j)
+            begin, room = sum(slots[:j]), slots[j]
             row = (CHUNK_ORDER[c] * stages + j) * 2 * LANES
 
             def pack(i, _):
@@ -292,14 +295,18 @@
                     if c < tiles:
                         packed[buf, k] = pool[c, at]
                     else:
-                        packed_row[j, pl.ds(k, 1), :] = pool_row[pl.ds(at, 1), :]
+                        packed_row[pl.ds(begin + k, 1), :] = pool_row[pl.ds(at, 1), :]
                 return 0
 
-            lax.fori_loop(0, slots // unroll, pack, 0)
+            lax.fori_loop(0, room // unroll, pack, 0)
             to = flip(d, 1 << bit)
             copy = pltpu.make_async_remote_copy(
-                src_ref=packed.at[buf] if c < tiles else packed_row.at[j],
-                dst_ref=landed.at[c, j] if c < tiles else landed_row.at[j],
+                src_ref=packed.at[buf, pl.ds(0, room)]
+                if c < tiles
+                else packed_row.at[pl.ds(begin, room)],
+                dst_ref=landed.at[c, pl.ds(begin, room)]
+                if c < tiles
+                else landed_row.at[pl.ds(begin, room)],
                 send_sem=send_sem.at[c, j],
                 recv_sem=recv_sem.at[c, j],
                 device_id=(to // peers, to % peers),
@@ -341,7 +348,7 @@
 def exchange(tables, finals, params, states, peers, own_blocks, slots):
     tiles = states.shape[0] // ROWS
     stages = len(ORDERS[0])
-    size = own_blocks + stages * slots
+    size = own_blocks + sum(slots)
     f32 = jnp.float32
     return pl.pallas_call(
         functools.partial(exchange_kernel, peers, own_blocks, slots, 8),
@@ -362,10 +369,10 @@
         scratch_shapes=[
             pltpu.VMEM((tiles, size, ROWS, LANES), f32),
             pltpu.VMEM((size, LANES), f32),
-            pltpu.VMEM((tiles, stages, slots, ROWS, LANES), f32),
-            pltpu.VMEM((stages, slots, LANES), f32),
-            pltpu.VMEM((8, slots, ROWS, LANES), f32),
-            pltpu.VMEM((stages, slots, LANES), f32),
+            pltpu.VMEM((tiles, sum(slots), ROWS, LANES), f32),
+            pltpu.VMEM((sum(slots), LANES), f32),
+            pltpu.VMEM((1 + max(max(b) for b in BUFFERS.values()), max(slots), ROWS, LANES), f32),
+            pltpu.VMEM((sum(slots), LANES), f32),
             pltpu.VMEM((own_blocks, ROWS, LANES), f32),
             pltpu.VMEM((own_blocks, LANES), f32),
             pltpu.SemaphoreType.DMA((tiles + 1, stages)),
@@ -466,12 +473,12 @@
         return general(gathered, devices, states, block_part, tile_perm, *gate_params)
     gathered = gather_counts(counts.reshape(1, 1, LANES), devices, peers)
     matrix = gathered[:, 0, :devices]
-    fits = largest_load(matrix, devices) <= SLOTS
+    fits = messages_fit(matrix, devices)
     tables, finals = make_tables(
         gathered, block_part.reshape(1, own_blocks), devices, peers, own_blocks, SLOTS
     )
     table_list = tables.reshape(-1)
-    final_list = finals[0:2].reshape(-1)
+    final_list = finals[0 : len(ORDERS)].reshape(-1)
     padded = jnp.stack([jnp.pad(p, (1, 0)) for p in gate_params])
     params = jnp.broadcast_to(padded[:, :, None], padded.shape + (LANES,))
 

time: 257 us -> 233 us (0.907)
  Pallas kernels: 245 us -> 221 us
    pallas_call x1, Pallas kernels: 225 us -> 201 us  [exchange(): pl.pallas_call(functools.partial(exchange_kernel, peers, own_blocks, slot...]
where the time goes in v2:
time: 233 us; the launch traced here: 229 us
  Pallas kernels  221 us (95%)
  local copies, waits for them, and re-layouts  3.58 us (2%)
  other arithmetic  2.6 us (1%)
    pallas_call x1, Pallas kernels, exchange(): pl.pallas_call(functools.partial(exchange_kernel, peers, own_blocks, slot...  201 us
    pallas_call x1, Pallas kernels, gather_counts(): pl.pallas_call(functools.partial(counts_kernel, devices, peers), out_shap...  8.77 us
    pallas_call x1, Pallas kernels, place(): pl.pallas_call(functools.partial(place_kernel, tiles, step), grid=(own_bl...  8.35 us

profile of v2, /device:TPU:25, one launch (start us, length us, event | category | flops | bytes accessed | tf_op | source)
XLA Modules:
  0.0 228.8 jit_solution(11040844380587666568)
XLA Ops:
  0.0 0.7 pad_bitcast_fusion.4
  0.7 1.3 convert_reduce_fusion
  2.0 0.7 pad_bitcast_fusion.2
  2.8 0.7 pad_bitcast_fusion
  3.6 8.8 %shard_map.111.c_ref = s32[32,1,128]{2,1,0:T(1,128)S(1)} custom-call(s32[1,1,128]{2,1,0:T(1,128)} %bitcast.77), custom_call_target="tpu_custom_call" | custom-call | tf_op jit(solution)/shard_map/pallas_call | solution.py:75
  12.3 1.2 fusion.6
  13.5 1.3 add_reduce_fusion
  15.5 2.9 %shard_map.112 = (s32[40,128]{1,0:T(8,128)}, s32[8,256]{1,0:T(8,128)S(1)}) custom-call(s32[32,1,128]{2,1,0:T(1,128)S(1)} %shard_map.111.c_ref, s32[1,256]{1,0:T(1,128)} %bitcast.75), custom_call_target="tpu_custom_call" | custom-call | tf_op jit(solution)/shard_map/pallas_call | solution.py:146
  18.4 210.5 %conditional.1 = (f32[41,32768]{1,0:T(8,128)}) conditional(s32[]{:T(128)} %convert_element_type.31, (s32[256]{0:T(256)}, s32[256,128]{1,0:T(8,128)}, s32[32,32]{1,0:T(8,128)S(1)}, f32[41,32768]{1,0:T(8,128)}, f32[40]{0:T(128)}, /*index=5*/f32[40]{0:T(128)}, f32[40]{0:T(128)}, f32[40]{0:T(128)}, f32[40]{0:T(128)}) %tuple.33, (s32[40,128]{1,0:T(8,128)}, ...), branch_computations={%region_3.11_spmd, %region_11.12_spmd} | conditional | flops 24065960 | bytes 187456160 | solution.py:494
  18.4 0.6 copy.55
  19.0 0.7 broadcast_in_dim.18.params
  19.7 200.8 %branch_1_fun.2 = (f32[5,256,8,128]{3,2,1,0:T(8,128)}, f32[256,128]{1,0:T(8,128)}) custom-call(s32[5120]{0:T(1024)} %bitcast.14.tables, s32[1024]{0:T(1024)} %bitcast.74, f32[5,41,128]{2,1,0:T(8,128)} %broadcast_in_dim.18.params, f32[41,32768]{1,0:T(8,128)} %get-tuple-element.52.states), custom_call_target="tpu_custom_call" | custom-call | tf_op jit(solution)/shard_map/cond/branch_1_fun/pallas_call | solution.py:353
  220.5 8.4 %branch_1_fun.3 = f32[41,32768]{1,0:T(8,128)} custom-call(f32[5,256,8,128]{3,2,1,0:T(8,128)} %get-tuple-element.53.got, f32[256,128]{1,0:T(8,128)} %get-tuple-element.54.got_row, s32[256,128]{1,0:T(8,128)} %get-tuple-element.55.perm), custom_call_target="tpu_custom_call" | custom-call | tf_op jit(solution)/shard_map/cond/branch_1_fun/pallas_call | solution.py:408
  (2 shorter events, 0.0 us)
